TPU v7x, 32 devices: a whole 2x2x4 slice. The times are simulated.
32 devices in a mesh: seq: 4 (over z), grp: 8 (over y, x, core).
Axes of the slice: x: 2, y: 2, z: 4, core: 2. Of those that a mesh axis runs over, the one named last changes fastest.
Arguments:
- hidden_in: bfloat16 [8, 2048, 1024], P('grp', 'seq'), may hold values from -64 to 64, as said below
- lengths: int32 [8], P('grp'), may hold values from 256 to 2048
- project_weight: bfloat16 [1024, 3072], replicated, may hold values from -0.1875 to 0.1875
- output_weight: bfloat16 [1024, 1024], replicated, may hold values from -0.1875 to 0.1875
- first_gain: float32 [1024], replicated, may hold values from 0.5 to 1.5
- first_shift: float32 [1024], replicated, may hold values from -3 to 3
- up_weight: bfloat16 [1024, 4096], P('grp'), may hold values from -0.1875 to 0.1875
- down_weight: bfloat16 [1024, 4096], P('grp'), may hold values from -0.09375 to 0.09375
- second_gain: float32 [1024], replicated, may hold values from 0.5 to 1.5
- second_shift: float32 [1024], replicated, may hold values from -3 to 3
- queries: float32 [64, 1024], P('grp'), may hold values from -6 to 6
- positive: int32 [64], P('grp'), may hold values from 0 to 7
Outputs:
- hidden_out: bfloat16 [8, 2048, 1024], P('grp', 'seq')
- embeddings: float32 [8, 1024], P('grp')
- query_loss: float32 [64], P('grp')
Inputs may be any that keep to these rules, and one draw needn't show every extreme that they name: `hidden_in`: activations.
All inputs are finite; a program needn't handle non-finite values.
Results may differ from a plain program's by a relative error of at most 0.0076.
Values may be sent and summed in bfloat16 or wider, within the bound.
A program may use at most 192 MiB of HBM per device.

v0:
```python
import math
import jax
import jax.numpy as jnp
from jax import lax
from jax.sharding import PartitionSpec as P

HEAD_DIM = 64


def layer_norm(values, gain, shift):
    average = jnp.mean(values, axis=-1, keepdims=True)
    centred = values - average
    variance = jnp.mean(centred * centred, axis=-1, keepdims=True)
    return centred * lax.rsqrt(variance + 1e-05) * gain + shift


def attend_local(gathered, length):
    seq_len = gathered.shape[0]
    local_width = gathered.shape[2]
    head_count = local_width // HEAD_DIM
    block = min(1024, seq_len)
    query_all = gathered[:, 0, :].reshape(seq_len, head_count, HEAD_DIM)
    key_all = gathered[:, 1, :].reshape(seq_len, head_count, HEAD_DIM)
    value_all = gathered[:, 2, :].reshape(seq_len, head_count, HEAD_DIM)
    key_valid = jnp.arange(seq_len, dtype=jnp.int32) < length
    scale = 1.0 / math.sqrt(HEAD_DIM)

    def one_block(index):
        query_rows = lax.dynamic_slice_in_dim(query_all, index * block, block, 0)
        scores = (
            jnp.einsum("qhd,khd->hqk", query_rows, key_all, preferred_element_type=jnp.float32)
            * scale
        )
        scores = jnp.where(key_valid[None, None, :], scores, -jnp.inf)
        highest = jnp.max(scores, axis=-1, keepdims=True)
        expo = jnp.exp(scores - highest)
        probs = (expo / jnp.sum(expo, axis=-1, keepdims=True)).astype(jnp.bfloat16)
        result = jnp.einsum("hqk,khd->qhd", probs, value_all, preferred_element_type=jnp.float32)
        return result.astype(jnp.bfloat16).reshape(block, local_width)

    blocks = lax.map(one_block, jnp.arange(seq_len // block, dtype=jnp.int32))
    return blocks.reshape(seq_len, local_width)


def group_weights(up_part, down_part):
    return (
        lax.all_gather(up_part, "grp", axis=0, tiled=True),
        lax.all_gather(down_part, "grp", axis=0, tiled=True),
    )


def expand_inner(rows_in, up_full):
    return jax.nn.gelu(
        jnp.dot(rows_in, up_full, preferred_element_type=jnp.float32), approximate=False
    ).astype(jnp.bfloat16)


def contract_down(inner_rows, down_full):
    return lax.dot_general(
        inner_rows, down_full, (((1,), (1,)), ((), ())), preferred_element_type=jnp.float32
    )


def body(
    hidden_in,
    lengths,
    project_weight,
    output_weight,
    first_gain,
    first_shift,
    up_weight,
    down_weight,
    second_gain,
    second_shift,
    queries,
    positive,
):
    tokens = hidden_in[0]
    tok_rows = tokens.shape[0]
    width = tokens.shape[1]
    rank = lax.axis_index("seq")
    length = lengths[0]
    projected = jnp.dot(tokens, project_weight, preferred_element_type=jnp.float32).astype(
        jnp.bfloat16
    )
    projected = projected.reshape(tok_rows, 3, width)
    gathered = lax.all_to_all(projected, "seq", split_axis=2, concat_axis=0, tiled=True)
    attended = attend_local(gathered, length)
    returned = lax.all_to_all(attended, "seq", split_axis=0, concat_axis=1, tiled=True)
    mixed = jnp.dot(returned, output_weight, preferred_element_type=jnp.float32)
    mixed = mixed + tokens.astype(jnp.float32)
    normed = layer_norm(mixed, first_gain, first_shift).astype(jnp.bfloat16)
    up_full, down_full = group_weights(up_weight, down_weight)
    inner = expand_inner(normed, up_full)
    outer = contract_down(inner, down_full)
    final = layer_norm(outer + normed.astype(jnp.float32), second_gain, second_shift)
    position = rank * tok_rows + jnp.arange(tok_rows, dtype=jnp.int32)
    valid = (position < length).astype(jnp.float32)
    local_total = jnp.sum(final * valid[:, None], axis=0)
    passage_total = lax.psum(local_total, "seq")
    pooled = passage_total / length.astype(jnp.float32)
    embedding = pooled / jnp.sqrt(jnp.sum(pooled * pooled) + 1e-06)
    short_passages = lax.all_gather(
        embedding.astype(jnp.bfloat16)[None, :], "grp", axis=0, tiled=True
    )
    short_queries = (
        queries / jnp.sqrt(jnp.sum(queries * queries, axis=-1, keepdims=True) + 1e-06)
    ).astype(jnp.bfloat16)
    logits = 20.0 * jnp.dot(short_queries, short_passages.T, preferred_element_type=jnp.float32)
    passage_ids = jnp.arange(short_passages.shape[0], dtype=jnp.int32)
    chosen = positive[:, None] == passage_ids[None, :]
    picked = jnp.sum(jnp.where(chosen, logits, 0.0), axis=1)
    query_loss = jnp.log(jnp.sum(jnp.exp(logits), axis=1)) - picked
    return (final.astype(jnp.bfloat16)[None], embedding[None, :], query_loss)


def solution(mesh):
    in_specs = (
        P("grp", "seq", None),
        P("grp"),
        P(),
        P(),
        P(),
        P(),
        P("grp", None),
        P("grp", None),
        P(),
        P(),
        P("grp", None),
        P("grp"),
    )
    out_specs = (P("grp", "seq", None), P("grp", None), P("grp"))
    return jax.shard_map(body, mesh=mesh, in_specs=in_specs, out_specs=out_specs, check_vma=False)
```

profile of v0, /device:TPU:0, one launch (start us, length us, event | category | flops | bytes accessed | tf_op | source)
XLA Modules:
  0.0 300.3 jit_solution(4461810352505724888)
XLA Ops:
  7.2 0.0 copy-start
  7.2 0.0 all-gather.4.cloned.1.call-start
  7.2 0.7 all-gather.4.cloned.1.call-update
  7.9 0.0 all-gather.6.cloned.1.call-start
  8.0 0.7 all-gather.6.cloned.1.call-update
  8.7 8.2 %convolution_convert_fusion = bf16[512,3072]{1,0:T(8,128)(2,1)} fusion(bf16[1024,3072]{1,0:T(8,128)(2,1)} %param.16, bf16[1,512,1024]{2,1,0:T(8,128)(2,1)} %param.14), kind=kOutput, calls=%fused_computation.44 | convolution fusion | flops 3222798336 | bytes 10485760 | tf_op jit(solution)/shard_map/dot_general | solution.py:83
  16.9 4.8 %copy.33 = bf16[512,3072]{0,1:T(8,128)(2,1)} copy(bf16[512,3072]{1,0:T(8,128)(2,1)} %convolution_convert_fusion) | data formatting | bytes 6291456 | tf_op jit(solution)/shard_map/convert_element_type | solution.py:83
  21.7 6.6 %copy.34 = bf16[512,3,1024]{0,1,2:T(4,128)(2,1)} copy(bf16[512,3,1024]{0,2,1:T(8,128)(2,1)} %bitcast.51) | data formatting | bytes 6291456 | tf_op jit(solution)/shard_map/reshape | solution.py:86
  28.3 6.3 %all-to-all-start = ((bf16[512,3,1024]{0,1,2:T(4,128)(2,1)}), bf16[512,3,1024]{0,1,2:T(4,128)(2,1)}, u32[]{:S(2)}, u32[]{:S(2)}) async-start(bf16[512,3,1024]{0,1,2:T(4,128)(2,1)} %copy.34), calls=%async_computation | async-start | bytes 8388608 | tf_op jit(solution)/shard_map/all_to_all | solution.py:87
  34.6 93.4 %all-to-all-done = bf16[512,3,1024]{0,1,2:T(4,128)(2,1)} async-done(((bf16[512,3,1024]{0,1,2:T(4,128)(2,1)}), bf16[512,3,1024]{0,1,2:T(4,128)(2,1)}, u32[]{:S(2)}, u32[]{:S(2)}) %all-to-all-start) | async-done | bytes 3145760 | tf_op jit(solution)/shard_map/all_to_all | solution.py:87
  128.0 4.7 %copy.35 = bf16[512,3,1024]{0,2,1:T(8,128)(2,1)} copy(bf16[512,3,1024]{0,1,2:T(4,128)(2,1)} %all-to-all-done) | data formatting | bytes 6291456 | tf_op jit(solution)/shard_map/all_to_all | solution.py:87
  132.7 4.7 %copy.36 = bf16[4,512,3,256]{3,1,0,2:T(8,128)(2,1)} copy(bf16[4,512,3,256]{1,3,0,2:T(8,128)(2,1)} %bitcast.52) | data formatting | bytes 6291456 | tf_op jit(solution)/shard_map/all_to_all | solution.py:87
  137.3 3.4 %fusion.97 = (bf16[2048,1,256]{2,0,1:T(8,128)(2,1)S(1)}, bf16[2048,1,256]{2,0,1:T(8,128)(2,1)}, bf16[2048,1,256]{2,0,1:T(8,128)(2,1)}) fusion(bf16[2048,3,256]{2,0,1:T(8,128)(2,1)} %bitcast.53), kind=kLoop, calls=%fused_computation.105 | loop fusion | bytes 6291456 | tf_op jit(solution)/shard_map/slice | solution.py:24
  140.8 2.3 copy.37
  143.1 2.3 copy.38
  145.3 1.4 copy.39
  146.8 52.2 %while.11 = (s32[]{:T(128)}, bf16[2,1024,256]{2,1,0:T(8,128)(2,1)}, s32[2]{0:T(128)S(1)}, bf16[2048,4,64]{0,2,1:T(8,128)(2,1)}, bf16[2048,4,64]{0,2,1:T(8,128)(2...) while((s32[]{:T(128)}, bf16[2,1024,256]{2,1,0:T(8,128)(2,1)}, ...), condition=%wide.region_3.4_spmd.clone, body=%wide.region_0.3_spmd.clone.sunk | while | flops 3296995328 | bytes 6855347 | solution.py:41
  146.8 0.6 dynamic_slice.31
  148.0 0.7 iota_compare_fusion.3
  148.7 11.0 %fusion.127 = f32[4,1024]{1,0:T(4,128)S(1)} fusion(pred[2048]{0:T(1024)(128)(4,1)S(1)} %iota_compare_fusion.3, bf16[2048,4,64]{0,2,1:T(8,128)(2,1)} %get-tuple-element.161, bf16[2048,4,64]{0,2,1:T(8,128)(2,1)} %get-tuple-element.160, s32[]{:T(128)S(6)} %select_n.42), kind=kOutput, calls=%fused_computation.104.clone.1 | convolution fusion | flops 1107298304 | bytes 1591300 | tf_op jit(solution)/shard_map/while/body/eval_jaxpr/sub | solution.py:36
  159.7 12.2 %fusion.128 = bf16[4,1024,64]{1,2,0:T(8,128)(2,1)S(1)} fusion(bf16[2048,4,64]{0,2,1:T(8,128)(2,1)} %get-tuple-element.162, f32[4,1024]{1,0:T(4,128)S(1)} %fusion.127, pred[2048]{0:T(1024)(128)(4,1)S(1)} %iota_compare_fusion.3, bf16[2048,4,64]{0,2,1:T(8,128)(2,1)} %get-tuple-element.161, bf16[2048,4,64]{0,2,1:T(8,128)(2,1)} %get-tuple-element.160, ...), kind=kOutput, calls=%fused_computation.11.clone.1 | convolution fusion | flops 2189694976 | bytes 3164164 | tf_op jit(solution)/shard_map/while/body/eval_jaxpr/hqk,khd->qhd/dot_general | solution.py:38
  171.8 0.2 copy.45
  172.0 0.8 constant_dynamic-update-slice_fusion.2
  172.9 0.6 dynamic_slice.31
  174.1 0.7 iota_compare_fusion.3
  174.8 11.0 %fusion.127 = f32[4,1024]{1,0:T(4,128)S(1)} fusion(pred[2048]{0:T(1024)(128)(4,1)S(1)} %iota_compare_fusion.3, bf16[2048,4,64]{0,2,1:T(8,128)(2,1)} %get-tuple-element.161, bf16[2048,4,64]{0,2,1:T(8,128)(2,1)} %get-tuple-element.160, s32[]{:T(128)S(6)} %select_n.42), kind=kOutput, calls=%fused_computation.104.clone.1 | convolution fusion | flops 1107298304 | bytes 1591300 | tf_op jit(solution)/shard_map/while/body/eval_jaxpr/sub | solution.py:36
  185.8 12.2 %fusion.128 = bf16[4,1024,64]{1,2,0:T(8,128)(2,1)S(1)} fusion(bf16[2048,4,64]{0,2,1:T(8,128)(2,1)} %get-tuple-element.162, f32[4,1024]{1,0:T(4,128)S(1)} %fusion.127, pred[2048]{0:T(1024)(128)(4,1)S(1)} %iota_compare_fusion.3, bf16[2048,4,64]{0,2,1:T(8,128)(2,1)} %get-tuple-element.161, bf16[2048,4,64]{0,2,1:T(8,128)(2,1)} %get-tuple-element.160, ...), kind=kOutput, calls=%fused_computation.11.clone.1 | convolution fusion | flops 2189694976 | bytes 3164164 | tf_op jit(solution)/shard_map/while/body/eval_jaxpr/hqk,khd->qhd/dot_general | solution.py:38
  197.9 0.2 copy.45
  198.1 0.8 constant_dynamic-update-slice_fusion.2
  199.0 3.6 %all-to-all-start.1 = ((bf16[4,512,256]{2,1,0:T(8,128)(2,1)}), bf16[4,512,256]{2,1,0:T(8,128)(2,1)S(1)}, u32[]{:S(2)}, u32[]{:S(2)}) async-start(bf16[4,512,256]{2,1,0:T(8,128)(2,1)} %bitcast.59), calls=%async_computation.1 | async-start | bytes 2097152 | tf_op jit(solution)/shard_map/all_to_all | solution.py:89
  203.3 0.1 multiply_reduce_fusion.3
  203.4 24.3 %all-to-all-done.1 = bf16[4,512,256]{2,1,0:T(8,128)(2,1)S(1)} async-done(((bf16[4,512,256]{2,1,0:T(8,128)(2,1)}), bf16[4,512,256]{2,1,0:T(8,128)(2,1)S(1)}, u32[]{:S(2)}, u32[]{:S(2)}) %all-to-all-start.1) | async-done | bytes 1048608 | tf_op jit(solution)/shard_map/all_to_all | solution.py:89
  227.8 1.3 copy.41
  229.1 2.9 fusion.98
  232.0 1.3 copy-done.1
  233.3 0.3 multiply_reduce_fusion.2
  233.7 0.0 copy-start.4
  233.7 0.0 all-gather.4.cloned.1.call-done
  233.7 0.0 all-gather.6.cloned.1.call-done
  233.8 33.2 %fusion.99 = (f32[512]{0:T(512)S(1)}, f32[512,1024]{1,0:T(8,128)}) fusion(f32[1024]{0:T(1024)S(1)} %copy-done.5, f32[1024]{0:T(1024)S(1)} %copy-done.6, f32[512]{0:T(512)S(1)} %add_rsqrt_fusion.1, f32[512,1024]{1,0:T(8,128)} %copy-done.1, f32[512]{0:T(512)S(1)} %broadcast_multiply_fusion.1, bf16[1024,4096]{1,0:T(8,128)(2,1)} %all-gather.6.cloned.1.call-done, ...), kind=kOutput, calls=%fused_computation.107 | convolution fusion | flops 8733065216 | bytes 20985856 | tf_op jit(solution)/shard_map/dot_general | solution.py:59
  267.0 1.9 multiply_reduce_fusion.1
  268.9 3.1 %multiply_reduce_fusion = (f32[1024]{0:T(1024)S(1)}, bf16[1,512,1024]{2,1,0:T(8,128)(2,1)}) fusion(f32[512,1024]{1,0:T(8,128)} %get-tuple-element.91, f32[512]{0:T(512)S(1)} %fusion.59, f32[1024]{0:T(1024)S(1)} %copy-done.3, f32[1024]{0:T(1024)S(1)} %copy-done.4, f32[512]{0:T(512)S(1)} %add_rsqrt_fusion, f32[512]{0:T(512)S(1)} %broadcast_multiply_fusion), kind=kLoop, calls=%fused_computation.46 | loop fusion | flops 3668992 | bytes 3164160 | tf_op jit(solution)/shard_map/reduce_sum | solution.py:99
  272.0 9.8 %psum.7 = f32[1024]{0:T(1024)S(1)} all-reduce(f32[1024]{0:T(1024)S(1)} %get-tuple-element.86), channel_id=1, replica_groups=mesh['seq'=4,'grp'=8] {'seq'}, use_global_device_ids=true, to_apply=%region_9.10 | all-reduce | flops 1024 | bytes 8192 | tf_op jit(solution)/shard_map/psum | solution.py:100
  281.8 0.6 multiply_reduce_fusion.4
  283.1 0.6 fusion.91
  283.7 9.0 %all-gather = bf16[8192]{0:T(1024)(128)(2,1)S(1)} all-gather(bf16[1024]{0:T(1024)(128)(2,1)S(1)} %get-tuple-element.81), channel_id=2, replica_groups=mesh['seq'=4,'grp'=8] {'grp'}, dimensions={0}, use_global_device_ids=true | all-gather | bytes 18432 | tf_op jit(solution)/shard_map/all_gather | solution.py:103
  292.7 0.2 exponential_reduce_fusion
  292.9 0.5 log_subtract_fusion
  (22 shorter events, 0.1 us)
Async XLA Ops:
  7.2 221.9 %copy-start = (bf16[1024,1024]{1,0:T(8,128)(2,1)S(1)}, bf16[1024,1024]{1,0:T(8,128)(2,1)}, u32[]{:S(2)}) copy-start(bf16[1024,1024]{1,0:T(8,128)(2,1)} %param.17) | copy-start | bytes 6291460
  7.2 226.6 %all-gather.4.cloned.1.call-start = ((), (), s32[]{:S(2)}) async-start(), calls=%async_computation.2 | async-start | bytes 9437184 | tf_op jit(solution)/shard_map/all_gather | solution.py:47
  7.9 225.8 %all-gather.6.cloned.1.call-start = ((), (), s32[]{:S(2)}) async-start(), calls=%async_computation.3 | async-start | bytes 9437184 | tf_op jit(solution)/shard_map/all_gather | solution.py:48
  28.3 99.7 %all-to-all-start = ((bf16[512,3,1024]{0,1,2:T(4,128)(2,1)}), bf16[512,3,1024]{0,1,2:T(4,128)(2,1)}, u32[]{:S(2)}, u32[]{:S(2)}) async-start(bf16[512,3,1024]{0,1,2:T(4,128)(2,1)} %copy.34), calls=%async_computation | async-start | bytes 8388608 | tf_op jit(solution)/shard_map/all_to_all | solution.py:87
  146.8 56.5 %copy-start.2 = (f32[8,1024]{1,0:T(8,128)S(1)}, f32[8,1024]{1,0:T(8,128)}, u32[]{:S(2)}) copy-start(f32[8,1024]{1,0:T(8,128)} %param.24) | copy-start | bytes 98308
  199.0 34.8 %copy-start.5 = (f32[1024]{0:T(1024)S(1)}, f32[1024]{0:T(1024)}, u32[]{:S(2)}) copy-start(f32[1024]{0:T(1024)} %param.19) | copy-start | bytes 12292
  199.0 34.8 %copy-start.6 = (f32[1024]{0:T(1024)S(1)}, f32[1024]{0:T(1024)}, u32[]{:S(2)}) copy-start(f32[1024]{0:T(1024)} %param.18) | copy-start | bytes 12292
  199.0 28.8 %all-to-all-start.1 = ((bf16[4,512,256]{2,1,0:T(8,128)(2,1)}), bf16[4,512,256]{2,1,0:T(8,128)(2,1)S(1)}, u32[]{:S(2)}, u32[]{:S(2)}) async-start(bf16[4,512,256]{2,1,0:T(8,128)(2,1)} %bitcast.59), calls=%async_computation.1 | async-start | bytes 2097152 | tf_op jit(solution)/shard_map/all_to_all | solution.py:89
  232.0 1.4 copy-start.1
  233.7 35.3 %copy-start.3 = (f32[1024]{0:T(1024)S(1)}, f32[1024]{0:T(1024)}, u32[]{:S(2)}) copy-start(f32[1024]{0:T(1024)} %param.23) | copy-start | bytes 12292
  233.7 35.3 %copy-start.4 = (f32[1024]{0:T(1024)S(1)}, f32[1024]{0:T(1024)}, u32[]{:S(2)}) copy-start(f32[1024]{0:T(1024)} %param.22) | copy-start | bytes 12292
  233.7 59.0 %copy-start.7 = (s32[8]{0:T(128)S(1)}, s32[8]{0:T(128)}, u32[]{:S(2)}) copy-start(s32[8]{0:T(128)} %param.25) | copy-start | bytes 100
Sparse Core Ops, SparseCore 0:
  9.9 56.9 all-gather.3
  68.8 54.2 all-gather.5
where the time goes:
time: 301 us; the launch traced here: 300 us
  waiting for transfers between devices  119 us (40%)
  matrix products  90.8 us (30%)
  local copies, waits for them, and re-layouts  36.1 us (12%)
  blocking collectives  18.7 us (6%)
  between operations  15.5 us (5%)
  starting transfers between devices  10 us (3%)
  other arithmetic  8.57 us (3%)
    all_to_all x1, waiting for transfers between devices, body(): lax.all_to_all(projected, 'seq', split_axis=2, concat_axis=0, tiled=True)  93.4 us
    dot_general x1, matrix products, contract_down(): lax.dot_general(inner_rows, down_full, (((1,), (1,)), ((), ())), preferre...  33.2 us
    all_to_all x1, waiting for transfers between devices, body(): lax.all_to_all(attended, 'seq', split_axis=0, concat_axis=1, tiled=True)  24.3 us
    dot_general x2, matrix products, one_block(): jnp.einsum('hqk,khd->qhd', probs, value_all, preferred_element_type=jnp.f...  24.3 us
    sub x2, matrix products, one_block(): expo = jnp.exp(scores - highest)  22 us
    psum x1, blocking collectives, body(): passage_total = lax.psum(local_total, 'seq')  9.76 us
    all_to_all x2, local copies, waits for them, and re-layouts, body(): lax.all_to_all(projected, 'seq', split_axis=2, concat_axis=0, tiled=True)  9.34 us
    all_gather x1, blocking collectives, body(): lax.all_gather(embedding.astype(jnp.bfloat16)[None, :], 'grp', axis=0, ti...  8.97 us
  transfers between devices with their start and end apart: 4, of which 2 were waited for; matrix products, arithmetic and copies ran while one was open for 31% of the time, Pallas kernels for 0%

commit v1 on v0

--- a/solution.py
+++ b/solution.py
@@ -84,7 +84,10 @@
         jnp.bfloat16
     )
     projected = projected.reshape(tok_rows, 3, width)
-    gathered = lax.all_to_all(projected, "seq", split_axis=2, concat_axis=0, tiled=True)
+    gathered = jnp.concatenate(
+        lax.all_to_all(jnp.stack(jnp.split(projected, lax.axis_size("seq"), axis=2)), "seq", 0, 0),
+        axis=0,
+    )
     attended = attend_local(gathered, length)
     returned = lax.all_to_all(attended, "seq", split_axis=0, concat_axis=1, tiled=True)
     mixed = jnp.dot(returned, output_weight, preferred_element_type=jnp.float32)

time: 301 us -> 271 us (0.900)
  waiting for transfers between devices: 119 us -> 96.6 us
  local copies, waits for them, and re-layouts: 36.1 us -> 27.1 us
    all_to_all x1, waiting for transfers between devices: 93.4 us -> 70.9 us  [body(): lax.all_to_all(jnp.stack(jnp.split(projected, lax.axis_size('seq'), axis=...]
    reshape x1 -> x0, local copies, waits for them, and re-layouts: 6.65 us -> none  [body(): projected = projected.reshape(tok_rows, 3, width)]
    all_to_all x2 -> x1, local copies, waits for them, and re-layouts: 9.34 us -> 4.69 us  [body(): lax.all_to_all(jnp.stack(jnp.split(projected, lax.axis_size('seq'), axis=...]
  transfers between devices with their start and end apart: 4 -> 4, of which waited for: 2 -> 2; matrix products, arithmetic and copies ran while one was open for 31% -> 32% of each run, Pallas kernels for 0% -> 0%
where the time goes in v1:
time: 271 us
  waiting for transfers between devices  96.6 us (36%)
  matrix products  90.8 us (34%)
  local copies, waits for them, and re-layouts  27.1 us (10%)
  blocking collectives  18.6 us (7%)
  between operations  15.5 us (6%)
  other arithmetic  10.4 us (4%)
  starting transfers between devices  10 us (4%)
    all_to_all x1, waiting for transfers between devices, body(): lax.all_to_all(jnp.stack(jnp.split(projected, lax.axis_size('seq'), axis=...  70.9 us
    dot_general x1, matrix products, contract_down(): lax.dot_general(inner_rows, down_full, (((1,), (1,)), ((), ())), preferre...  33.2 us
    dot_general x2, matrix products, one_block(): jnp.einsum('hqk,khd->qhd', probs, value_all, preferred_element_type=jnp.f...  24.3 us
    all_to_all x1, waiting for transfers between devices, body(): lax.all_to_all(attended, 'seq', split_axis=0, concat_axis=1, tiled=True)  24.3 us
    sub x2, matrix products, one_block(): expo = jnp.exp(scores - highest)  22 us
    psum x1, blocking collectives, body(): passage_total = lax.psum(local_total, 'seq')  9.76 us
    all_gather x1, blocking collectives, body(): lax.all_gather(embedding.astype(jnp.bfloat16)[None, :], 'grp', axis=0, ti...  8.89 us
    dot_general x1, matrix products, body(): jnp.dot(tokens, project_weight, preferred_element_type=jnp.float32)  8.21 us
  transfers between devices with their start and end apart: 4, of which 2 were waited for; matrix products, arithmetic and copies ran while one was open for 32% of the time, Pallas kernels for 0%

profile of v1, /device:TPU:0, one launch (start us, length us, event | category | flops | bytes accessed | tf_op | source)
XLA Modules:
  0.0 270.5 jit_solution(476706529264340565)
XLA Ops:
  7.2 0.0 copy-start
  7.2 0.0 all-gather.4.cloned.1.call-start
  7.2 0.7 all-gather.4.cloned.1.call-update
  7.9 0.0 all-gather.6.cloned.1.call-start
  8.0 0.7 all-gather.6.cloned.1.call-update
  8.7 8.2 %convolution_convert_fusion = bf16[512,3072]{1,0:T(8,128)(2,1)} fusion(bf16[1024,3072]{1,0:T(8,128)(2,1)} %param.16, bf16[1,512,1024]{2,1,0:T(8,128)(2,1)} %param.14), kind=kOutput, calls=%fused_computation.44 | convolution fusion | flops 3222798336 | bytes 10485760 | tf_op jit(solution)/shard_map/dot_general | solution.py:83
  16.9 4.8 %copy.35 = bf16[512,3072]{0,1:T(8,128)(2,1)} copy(bf16[512,3072]{1,0:T(8,128)(2,1)} %convolution_convert_fusion) | data formatting | bytes 6291456 | tf_op jit(solution)/shard_map/convert_element_type | solution.py:83
  21.7 2.1 slice_bitcast_fusion.3
  23.8 1.9 pad_maximum_fusion
  25.7 6.3 %all-to-all-start = ((bf16[4,512,3,256]{1,3,2,0:T(8,128)(2,1)}), bf16[4,512,3,256]{1,3,2,0:T(8,128)(2,1)}, u32[]{:S(2)}, u32[]{:S(2)}) async-start(bf16[4,512,3,256]{1,3,2,0:T(8,128)(2,1)} %pad_maximum_fusion), calls=%async_computation | async-start | bytes 6291456 | tf_op jit(solution)/shard_map/all_to_all | solution.py:88
  32.0 70.9 %all-to-all-done = bf16[4,512,3,256]{1,3,2,0:T(8,128)(2,1)} async-done(((bf16[4,512,3,256]{1,3,2,0:T(8,128)(2,1)}), bf16[4,512,3,256]{1,3,2,0:T(8,128)(2,1)}, u32[]{:S(2)}, u32[]{:S(2)}) %all-to-all-start) | async-done | bytes 3145760 | tf_op jit(solution)/shard_map/all_to_all | solution.py:88
  102.9 4.7 %copy.36 = bf16[4,512,3,256]{3,1,0,2:T(8,128)(2,1)} copy(bf16[4,512,3,256]{1,3,2,0:T(8,128)(2,1)} %all-to-all-done) | data formatting | bytes 6291456 | tf_op jit(solution)/shard_map/all_to_all | solution.py:88
  107.6 3.5 %fusion.97 = (bf16[2048,1,256]{2,0,1:T(8,128)(2,1)S(1)}, bf16[2048,1,256]{2,0,1:T(8,128)(2,1)}, bf16[2048,1,256]{2,0,1:T(8,128)(2,1)}) fusion(bf16[2048,3,256]{2,0,1:T(8,128)(2,1)} %bitcast.57), kind=kLoop, calls=%fused_computation.110 | loop fusion | bytes 6291456 | tf_op jit(solution)/shard_map/slice | solution.py:24
  111.0 2.3 copy.37
  113.3 2.3 copy.38
  115.6 1.4 copy.39
  117.1 52.2 %while.11 = (s32[]{:T(128)}, bf16[2,1024,256]{2,1,0:T(8,128)(2,1)}, s32[2]{0:T(128)S(1)}, bf16[2048,4,64]{0,2,1:T(8,128)(2,1)}, bf16[2048,4,64]{0,2,1:T(8,128)(2...) while((s32[]{:T(128)}, bf16[2,1024,256]{2,1,0:T(8,128)(2,1)}, ...), condition=%wide.region_3.4_spmd.clone, body=%wide.region_0.3_spmd.clone.sunk | while | flops 3296995328 | bytes 6855347 | solution.py:41
  117.1 0.6 dynamic_slice.31
  118.3 0.7 iota_compare_fusion.3
  119.0 11.0 %fusion.127 = f32[4,1024]{1,0:T(4,128)S(1)} fusion(pred[2048]{0:T(1024)(128)(4,1)S(1)} %iota_compare_fusion.3, bf16[2048,4,64]{0,2,1:T(8,128)(2,1)} %get-tuple-element.165, bf16[2048,4,64]{0,2,1:T(8,128)(2,1)} %get-tuple-element.164, s32[]{:T(128)S(6)} %select_n.42), kind=kOutput, calls=%fused_computation.109.clone.1 | convolution fusion | flops 1107298304 | bytes 1591300 | tf_op jit(solution)/shard_map/while/body/eval_jaxpr/sub | solution.py:36
  130.0 12.2 %fusion.128 = bf16[4,1024,64]{1,2,0:T(8,128)(2,1)S(1)} fusion(bf16[2048,4,64]{0,2,1:T(8,128)(2,1)} %get-tuple-element.166, f32[4,1024]{1,0:T(4,128)S(1)} %fusion.127, pred[2048]{0:T(1024)(128)(4,1)S(1)} %iota_compare_fusion.3, bf16[2048,4,64]{0,2,1:T(8,128)(2,1)} %get-tuple-element.165, bf16[2048,4,64]{0,2,1:T(8,128)(2,1)} %get-tuple-element.164, ...), kind=kOutput, calls=%fused_computation.11.clone.1 | convolution fusion | flops 2189694976 | bytes 3164164 | tf_op jit(solution)/shard_map/while/body/eval_jaxpr/hqk,khd->qhd/dot_general | solution.py:38
  142.2 0.2 copy.45
  142.4 0.8 constant_dynamic-update-slice_fusion.2
  143.2 0.6 dynamic_slice.31
  144.4 0.7 iota_compare_fusion.3
  145.1 11.0 %fusion.127 = f32[4,1024]{1,0:T(4,128)S(1)} fusion(pred[2048]{0:T(1024)(128)(4,1)S(1)} %iota_compare_fusion.3, bf16[2048,4,64]{0,2,1:T(8,128)(2,1)} %get-tuple-element.165, bf16[2048,4,64]{0,2,1:T(8,128)(2,1)} %get-tuple-element.164, s32[]{:T(128)S(6)} %select_n.42), kind=kOutput, calls=%fused_computation.109.clone.1 | convolution fusion | flops 1107298304 | bytes 1591300 | tf_op jit(solution)/shard_map/while/body/eval_jaxpr/sub | solution.py:36
  156.1 12.2 %fusion.128 = bf16[4,1024,64]{1,2,0:T(8,128)(2,1)S(1)} fusion(bf16[2048,4,64]{0,2,1:T(8,128)(2,1)} %get-tuple-element.166, f32[4,1024]{1,0:T(4,128)S(1)} %fusion.127, pred[2048]{0:T(1024)(128)(4,1)S(1)} %iota_compare_fusion.3, bf16[2048,4,64]{0,2,1:T(8,128)(2,1)} %get-tuple-element.165, bf16[2048,4,64]{0,2,1:T(8,128)(2,1)} %get-tuple-element.164, ...), kind=kOutput, calls=%fused_computation.11.clone.1 | convolution fusion | flops 2189694976 | bytes 3164164 | tf_op jit(solution)/shard_map/while/body/eval_jaxpr/hqk,khd->qhd/dot_general | solution.py:38
  168.3 0.2 copy.45
  168.5 0.8 constant_dynamic-update-slice_fusion.2
  169.3 3.6 %all-to-all-start.1 = ((bf16[4,512,256]{2,1,0:T(8,128)(2,1)}), bf16[4,512,256]{2,1,0:T(8,128)(2,1)S(1)}, u32[]{:S(2)}, u32[]{:S(2)}) async-start(bf16[4,512,256]{2,1,0:T(8,128)(2,1)} %bitcast.63), calls=%async_computation.1 | async-start | bytes 2097152 | tf_op jit(solution)/shard_map/all_to_all | solution.py:92
  173.6 0.1 multiply_reduce_fusion.3
  173.8 24.3 %all-to-all-done.1 = bf16[4,512,256]{2,1,0:T(8,128)(2,1)S(1)} async-done(((bf16[4,512,256]{2,1,0:T(8,128)(2,1)}), bf16[4,512,256]{2,1,0:T(8,128)(2,1)S(1)}, u32[]{:S(2)}, u32[]{:S(2)}) %all-to-all-start.1) | async-done | bytes 1048608 | tf_op jit(solution)/shard_map/all_to_all | solution.py:92
  198.1 1.3 copy.41
  199.4 2.9 %fusion.98 = (f32[512]{0:T(512)S(1)}, f32[512,1024]{1,0:T(8,128)S(1)}) fusion(bf16[1,512,1024]{2,1,0:T(8,128)(2,1)} %param.14, bf16[512,1024]{0,1:T(8,128)(2,1)} %bitcast.59, bf16[1024,1024]{1,0:T(8,128)(2,1)S(1)} %copy-done), kind=kOutput, calls=%fused_computation.111 | convolution fusion | flops 1075314176 | bytes 6293504 | tf_op jit(solution)/shard_map/dot_general | solution.py:93
  202.3 1.3 copy-done.1
  203.6 0.3 multiply_reduce_fusion.2
  204.0 0.0 copy-start.7
  204.0 0.0 all-gather.4.cloned.1.call-done
  204.1 0.0 all-gather.6.cloned.1.call-done
  204.1 33.2 %fusion.99 = (f32[512]{0:T(512)S(1)}, f32[512,1024]{1,0:T(8,128)}) fusion(f32[1024]{0:T(1024)S(1)} %copy-done.5, f32[1024]{0:T(1024)S(1)} %copy-done.6, f32[512]{0:T(512)S(1)} %add_rsqrt_fusion.1, f32[512,1024]{1,0:T(8,128)} %copy-done.1, f32[512]{0:T(512)S(1)} %broadcast_multiply_fusion.1, bf16[1024,4096]{1,0:T(8,128)(2,1)} %all-gather.6.cloned.1.call-done, ...), kind=kOutput, calls=%fused_computation.112 | convolution fusion | flops 8733065216 | bytes 20985856 | tf_op jit(solution)/shard_map/dot_general | solution.py:59
  237.3 1.9 multiply_reduce_fusion.1
  239.3 3.1 %multiply_reduce_fusion = (f32[1024]{0:T(1024)S(1)}, bf16[1,512,1024]{2,1,0:T(8,128)(2,1)}) fusion(f32[512,1024]{1,0:T(8,128)} %get-tuple-element.95, f32[512]{0:T(512)S(1)} %fusion.59, f32[1024]{0:T(1024)S(1)} %copy-done.3, f32[1024]{0:T(1024)S(1)} %copy-done.4, f32[512]{0:T(512)S(1)} %add_rsqrt_fusion, f32[512]{0:T(512)S(1)} %broadcast_multiply_fusion), kind=kLoop, calls=%fused_computation.47 | loop fusion | flops 3668992 | bytes 3164160 | tf_op jit(solution)/shard_map/reduce_sum | solution.py:102
  242.4 9.8 %psum.7 = f32[1024]{0:T(1024)S(1)} all-reduce(f32[1024]{0:T(1024)S(1)} %get-tuple-element.90), channel_id=1, replica_groups=mesh['seq'=4,'grp'=8] {'seq'}, use_global_device_ids=true, to_apply=%region_9.10 | all-reduce | flops 1024 | bytes 8192 | tf_op jit(solution)/shard_map/psum | solution.py:103
  252.1 0.6 multiply_reduce_fusion.4
  253.4 0.6 fusion.91
  254.0 8.9 %all-gather = bf16[8192]{0:T(1024)(128)(2,1)S(1)} all-gather(bf16[1024]{0:T(1024)(128)(2,1)S(1)} %get-tuple-element.81), channel_id=2, replica_groups=mesh['seq'=4,'grp'=8] {'grp'}, dimensions={0}, use_global_device_ids=true | all-gather | bytes 18432 | tf_op jit(solution)/shard_map/all_gather | solution.py:106
  262.9 0.2 exponential_reduce_fusion
  263.2 0.5 log_subtract_fusion
  (22 shorter events, 0.1 us)
Async XLA Ops:
  7.2 192.2 %copy-start = (bf16[1024,1024]{1,0:T(8,128)(2,1)S(1)}, bf16[1024,1024]{1,0:T(8,128)(2,1)}, u32[]{:S(2)}) copy-start(bf16[1024,1024]{1,0:T(8,128)(2,1)} %param.17) | copy-start | bytes 6291460
  7.2 196.9 %all-gather.4.cloned.1.call-start = ((), (), s32[]{:S(2)}) async-start(), calls=%async_computation.2 | async-start | bytes 9437184 | tf_op jit(solution)/shard_map/all_gather | solution.py:47
  7.9 196.2 %all-gather.6.cloned.1.call-start = ((), (), s32[]{:S(2)}) async-start(), calls=%async_computation.3 | async-start | bytes 9437184 | tf_op jit(solution)/shard_map/all_gather | solution.py:48
  25.7 77.2 %all-to-all-start = ((bf16[4,512,3,256]{1,3,2,0:T(8,128)(2,1)}), bf16[4,512,3,256]{1,3,2,0:T(8,128)(2,1)}, u32[]{:S(2)}, u32[]{:S(2)}) async-start(bf16[4,512,3,256]{1,3,2,0:T(8,128)(2,1)} %pad_maximum_fusion), calls=%async_computation | async-start | bytes 6291456 | tf_op jit(solution)/shard_map/all_to_all | solution.py:88
  117.1 56.6 %copy-start.2 = (f32[8,1024]{1,0:T(8,128)S(1)}, f32[8,1024]{1,0:T(8,128)}, u32[]{:S(2)}) copy-start(f32[8,1024]{1,0:T(8,128)} %param.24) | copy-start | bytes 98308
  169.3 34.8 %copy-start.5 = (f32[1024]{0:T(1024)S(1)}, f32[1024]{0:T(1024)}, u32[]{:S(2)}) copy-start(f32[1024]{0:T(1024)} %param.19) | copy-start | bytes 12292
  169.3 34.8 %copy-start.6 = (f32[1024]{0:T(1024)S(1)}, f32[1024]{0:T(1024)}, u32[]{:S(2)}) copy-start(f32[1024]{0:T(1024)} %param.18) | copy-start | bytes 12292
  169.3 28.8 %all-to-all-start.1 = ((bf16[4,512,256]{2,1,0:T(8,128)(2,1)}), bf16[4,512,256]{2,1,0:T(8,128)(2,1)S(1)}, u32[]{:S(2)}, u32[]{:S(2)}) async-start(bf16[4,512,256]{2,1,0:T(8,128)(2,1)} %bitcast.63), calls=%async_computation.1 | async-start | bytes 2097152 | tf_op jit(solution)/shard_map/all_to_all | solution.py:92
  202.3 1.4 copy-start.1
  204.0 35.3 %copy-start.3 = (f32[1024]{0:T(1024)S(1)}, f32[1024]{0:T(1024)}, u32[]{:S(2)}) copy-start(f32[1024]{0:T(1024)} %param.23) | copy-start | bytes 12292
  204.0 35.3 %copy-start.4 = (f32[1024]{0:T(1024)S(1)}, f32[1024]{0:T(1024)}, u32[]{:S(2)}) copy-start(f32[1024]{0:T(1024)} %param.22) | copy-start | bytes 12292
  204.0 58.9 %copy-start.7 = (s32[8]{0:T(128)S(1)}, s32[8]{0:T(128)}, u32[]{:S(2)}) copy-start(s32[8]{0:T(128)} %param.25) | copy-start | bytes 100
Sparse Core Ops, SparseCore 0:
  9.9 56.9 all-gather.3
  68.8 54.2 all-gather.5
